TPU v7x, 512 devices: a whole 4x8x8 slice. The times are simulated.
512 devices in a mesh: dp: 8 (over x, core), vocab: 64 (over y, z).
Axes of the slice: x: 4, y: 8, z: 8, core: 2. Of those that a mesh axis runs over, the one named last changes fastest.
Arguments:
- hidden: bfloat16 [1792, 4608], P('dp'), may hold values from -15 to 15
- out_weight: bfloat16 [4608, 24576], P('dp', 'vocab'), may hold values from -0.09375 to 0.09375
- targets: int32 [1792], P('dp'), may hold values from 0 to 24383
- token_weight: float32 [1792], P('dp'), may hold values from 0.3 to 3
Outputs:
- token_loss: float32 [1792], P('dp')
- hidden_grad: bfloat16 [1792, 4608], P('dp')
- weight_grad: bfloat16 [4608, 24576], P('dp', 'vocab')
All inputs are finite; a program needn't handle non-finite values.
Results may differ from a plain program's by a relative error of at most 0.0085.
Values may be sent and summed in bfloat16 or wider, within the bound.
A program may use at most 64 MiB of HBM per device.

v0:
```python
import jax
import jax.numpy as jnp
from jax import lax
from jax.sharding import Mesh
from jax.sharding import PartitionSpec as P

VOCAB = ("vocab_0", "vocab_1")
softcap = 30.0


def by_axis(array, axes):
    for axis in axes:
        array = lax.psum(array, axis)
    return array


def in_blocks(array, dim, peers):
    before, after = (array.shape[:dim], array.shape[dim + 1 :])
    return jnp.moveaxis(array.reshape(*before, peers, -1, *after), dim, 0)


def sent_and_summed(array, axis, dim):
    blocks = in_blocks(array, dim, lax.axis_size(axis))
    arrived = lax.all_to_all(blocks, axis, split_axis=0, concat_axis=0, tiled=True)
    return arrived.astype(jnp.float32).sum(axis=0)


def from_everyone(array, axis):
    peers = lax.axis_size(axis)
    return lax.all_to_all(
        jnp.broadcast_to(array[None], (peers, *array.shape)), axis, 0, 0, tiled=True
    )


def in_order(blocks, dim):
    blocks = jnp.moveaxis(blocks, 0, dim)
    lengths = blocks.shape
    return blocks.reshape(*lengths[:dim], lengths[dim] * lengths[dim + 1], *lengths[dim + 2 :])


def gather_directly(array, axis, dim):
    blocks = from_everyone(array, axis)
    return in_order(blocks, dim)


def body(hidden, out_weight, targets, token_weight):
    shard_width = out_weight.shape[1]
    row_count = out_weight.shape[0]
    tok_rows = hidden.shape[0]
    vocab_used = shard_width * lax.axis_size(VOCAB) - shard_width // 2
    first_col = lax.axis_index(VOCAB) * shard_width
    col_ids = first_col + jnp.arange(shard_width, dtype=jnp.int32)
    usable = col_ids < vocab_used
    w_full = lax.all_gather(out_weight, "dp", axis=0, tiled=True)
    logits = jnp.dot(hidden, w_full, preferred_element_type=jnp.float32)
    squash = jnp.tanh(logits / softcap)
    capped = softcap * squash
    exp_terms = jnp.where(usable[None, :], jnp.exp(capped), jnp.float32(0.0))
    target_hit = col_ids[None, :] == targets[:, None]
    local_sum = jnp.sum(exp_terms, axis=1)
    local_target = jnp.sum(jnp.where(target_hit, capped, jnp.float32(0.0)), axis=1)
    sums, target_logit = (by_axis(local_sum, VOCAB), by_axis(local_target, VOCAB))
    token_loss = jnp.log(sums) - target_logit
    onehot = jnp.where(target_hit, jnp.float32(1.0), jnp.float32(0.0))
    logit_grad = (
        token_weight[:, None] * (exp_terms / sums[:, None] - onehot) * (1.0 - squash * squash)
    ).astype(jnp.bfloat16)
    contract_cols = (((1,), (1,)), ((), ()))
    partial_grad = lax.dot_general(
        logit_grad, w_full, contract_cols, preferred_element_type=jnp.float32
    )
    share = sent_and_summed(partial_grad.astype(jnp.bfloat16), VOCAB, 1).astype(jnp.bfloat16)
    hidden_grad = lax.all_gather(share, VOCAB, axis=1, tiled=True)
    owned_cols = lax.all_to_all(hidden, "dp", split_axis=1, concat_axis=0, tiled=True)
    every_grad = gather_directly(logit_grad, "dp", 0)
    block_count = owned_cols.shape[0] // tok_rows
    col_blocks = owned_cols.reshape(block_count, tok_rows, row_count)
    grad_blocks = every_grad.reshape(block_count, tok_rows, shard_width)
    block_terms = jnp.einsum(
        "ntr,ntv->nrv", col_blocks, grad_blocks, preferred_element_type=jnp.float32
    ).astype(jnp.bfloat16)
    weight_grad = jnp.sum(block_terms.astype(jnp.float32), axis=0).astype(jnp.bfloat16)
    return (token_loss, hidden_grad, weight_grad)


def solution(mesh):
    torus = Mesh(mesh.devices.reshape(mesh.shape["dp"], 8, 8), ("dp", "vocab_0", "vocab_1"))
    in_specs = (P("dp", None), P("dp", VOCAB), P("dp"), P("dp"))
    out_specs = (P("dp"), P("dp", None), P("dp", VOCAB))
    return jax.shard_map(body, mesh=torus, in_specs=in_specs, out_specs=out_specs, check_vma=False)
```

profile of v0, /device:TPU:4, one launch (start us, length us, event | category | flops | bytes accessed | tf_op | source)
XLA Modules:
  0.0 244.0 jit_solution(11273807396610826851)
XLA Ops:
  7.2 0.0 all-gather.3.cloned.1.call-start
  7.2 0.7 all-gather.3.cloned.1.call-update
  7.9 0.0 all-gather.5.cloned.1.call-start
  8.0 0.0 copy-start.1
  8.0 40.0 %all-gather.3.cloned.1.call-done = bf16[4608,384]{1,0:T(8,128)(2,1)} async-done(((bf16[576,384]{1,0:T(8,128)(2,1)}), bf16[4608,384]{1,0:T(8,128)(2,1)}) %all-gather.3.cloned.1.call-update) | async-done | bytes 3538960 | tf_op jit(solution)/shard_map/all_gather | solution.py:54
  48.0 4.1 %fusion.7 = (f32[224]{0:T(256)S(1)}, f32[224]{0:T(256)S(1)}, f32[224,384]{1,0:T(8,128)S(1)}) fusion(pred[384]{0:T(512)(128)(4,1)S(1)} %broadcast_compare_fusion, s32[224]{0:T(256)} %param.6, s32[384]{0:T(512)S(1)} %iota_add_fusion, bf16[224,4608]{1,0:T(8,128)(2,1)} %param.4, bf16[4608,384]{1,0:T(8,128)(2,1)} %all-gather.3.cloned.1.call-done), kind=kOutput, calls=%fused_computation.13 | convolution fusion | flops 793325056 | bytes 5952000 | tf_op jit(solution)/shard_map/dot_general | solution.py:55
  52.1 17.0 %all-reduce.1 = (f32[224]{0:T(256)S(1)}, f32[224]{0:T(256)S(1)}) all-reduce(f32[224]{0:T(256)S(1)} %get-tuple-element.7, f32[224]{0:T(256)S(1)} %get-tuple-element.6), channel_id=1, replica_groups=mesh['dp'=8,'vocab_0'=8,'vocab_1'=8] {'vocab_0'}, use_global_device_ids=true, to_apply=%region_4.5 | all-reduce | flops 448 | bytes 3584 | tf_op jit(solution)/shard_map/psum | solution.py:13
  69.1 18.1 %all-reduce = (f32[224]{0:T(256)S(1)}, f32[224]{0:T(256)S(1)}) all-reduce(f32[224]{0:T(256)S(1)} %get-tuple-element.10, f32[224]{0:T(256)S(1)} %get-tuple-element.11), channel_id=1, replica_groups=mesh['dp'=8,'vocab_0'=8,'vocab_1'=8] {'vocab_1'}, use_global_device_ids=true, to_apply=%region_5.6 | all-reduce | flops 448 | bytes 3584 | tf_op jit(solution)/shard_map/psum | solution.py:13
  87.2 0.2 fusion.6
  87.4 3.4 %convolution_convert_fusion = bf16[224,4608]{1,0:T(8,128)(2,1)S(1)} fusion(bf16[224,384]{1,0:T(8,128)(2,1)S(1)} %fusion.6, bf16[4608,384]{1,0:T(8,128)(2,1)} %all-gather.3.cloned.1.call-done), kind=kOutput, calls=%fused_computation | convolution fusion | flops 793755648 | bytes 5775360 | tf_op jit(solution)/shard_map/dot_general | solution.py:69
  90.8 2.4 copy.9
  93.2 60.9 %all_to_all.26 = bf16[64,224,72]{1,2,0:T(8,128)(2,1)S(1)} all-to-all(bf16[64,224,72]{1,2,0:T(8,128)(2,1)} %bitcast.12), channel_id=1, replica_groups=mesh['dp'=8,'vocab_0'=8,'vocab_1'=8] {'vocab_0','vocab_1'}, dimensions={0} | all-to-all | bytes 4128768 | tf_op jit(solution)/shard_map/all_to_all | solution.py:24
  154.1 1.0 reduce_sum.46
  155.1 0.0 all-gather.5.cloned.1.call-update
  155.1 3.6 %all_to_all.20 = bf16[224,8,576]{2,1,0:T(8,128)(2,1)S(1)} reshape(bf16[224,4608]{1,0:T(8,128)(2,1)} %param.4) | data formatting | bytes 4128768 | tf_op jit(solution)/shard_map/all_to_all | solution.py:74
  158.7 0.3 copy.10
  159.0 31.3 %all_to_all.27 = bf16[224,8,576]{2,0,1:T(8,128)(2,1)S(1)} all-to-all(bf16[224,8,576]{2,0,1:T(8,128)(2,1)S(1)} %copy.10), channel_id=1, replica_groups=mesh['dp'=8,'vocab_0'=8,'vocab_1'=8] {'dp'}, dimensions={1} | all-to-all | bytes 4128768 | tf_op jit(solution)/shard_map/all_to_all | solution.py:74
  190.2 1.2 broadcast_in_dim.34
  191.4 6.8 %all-to-all-start.1 = ((bf16[8,224,384]{2,1,0:T(8,128)(2,1)}), bf16[8,224,384]{2,1,0:T(8,128)(2,1)}, u32[]{:S(2)}, u32[]{:S(2)}) async-start(bf16[8,224,384]{2,1,0:T(8,128)(2,1)} %broadcast_in_dim.34), calls=%async_computation.1 | async-start | bytes 2752512 | tf_op jit(solution)/shard_map/all_to_all | solution.py:30
  198.3 0.6 log_subtract_fusion
  198.8 15.8 %all-to-all-done.1 = bf16[8,224,384]{2,1,0:T(8,128)(2,1)} async-done(((bf16[8,224,384]{2,1,0:T(8,128)(2,1)}), bf16[8,224,384]{2,1,0:T(8,128)(2,1)}, u32[]{:S(2)}, u32[]{:S(2)}) %all-to-all-start.1) | async-done | bytes 1376288 | tf_op jit(solution)/shard_map/all_to_all | solution.py:30
  214.7 3.6 %convert_reduce_fusion = bf16[384,576]{0,1:T(8,128)(2,1)} fusion(bf16[8,224,384]{2,1,0:T(8,128)(2,1)} %all-to-all-done.1, bf16[224,8,576]{2,0,1:T(8,128)(2,1)S(1)} %all_to_all.27), kind=kOutput, calls=%fused_computation.1 | convolution fusion | flops 796041216 | bytes 3883008 | tf_op jit(solution)/shard_map/ntr,ntv->nrv/dot_general | solution.py:79
  218.3 14.7 %all-gather.5.cloned.1.call-done = bf16[224,4608]{0,1:T(8,128)(2,1)} async-done(((bf16[224,72]{0,1:T(8,128)(2,1)}), bf16[224,4608]{0,1:T(8,128)(2,1)}) %all-gather.5.cloned.1.call-update) | async-done | bytes 2064400 | tf_op jit(solution)/shard_map/all_gather | solution.py:73
  233.0 4.1 %copy.11 = bf16[224,4608]{1,0:T(8,128)(2,1)} copy(bf16[224,4608]{0,1:T(8,128)(2,1)} %all-gather.5.cloned.1.call-done) | data formatting | bytes 4128768
  (5 shorter events, 0.0 us)
Async XLA Ops:
  7.2 40.9 %all-gather.3.cloned.1.call-start = ((), (), s32[]{:S(2)}) async-start(), calls=%async_computation.3 | async-start | bytes 3981312 | tf_op jit(solution)/shard_map/all_gather | solution.py:54
  7.9 225.1 %all-gather.5.cloned.1.call-start = ((), (), s32[]{:S(2)}) async-start(), calls=%async_computation.4 | async-start | bytes 2396160 | tf_op jit(solution)/shard_map/all_gather | solution.py:73
  8.0 79.2 %copy-start = (s32[224]{0:T(256)S(1)}, s32[224]{0:T(256)}, u32[]{:S(2)}) copy-start(s32[224]{0:T(256)} %param.6) | copy-start | bytes 2692
  8.0 79.2 %copy-start.1 = (f32[224]{0:T(256)S(1)}, f32[224]{0:T(256)}, u32[]{:S(2)}) copy-start(f32[224]{0:T(256)} %param.7) | copy-start | bytes 2692
  191.4 23.2 %all-to-all-start.1 = ((bf16[8,224,384]{2,1,0:T(8,128)(2,1)}), bf16[8,224,384]{2,1,0:T(8,128)(2,1)}, u32[]{:S(2)}, u32[]{:S(2)}) async-start(bf16[8,224,384]{2,1,0:T(8,128)(2,1)} %broadcast_in_dim.34), calls=%async_computation.1 | async-start | bytes 2752512 | tf_op jit(solution)/shard_map/all_to_all | solution.py:30
Sparse Core Ops, SparseCore 0:
  10.1 37.8 all-gather.2
  155.2 77.6 all-gather.4
where the time goes:
time: 244 us
  blocking collectives  127 us (52%)
  waiting for transfers between devices  71.2 us (29%)
  between operations  14.1 us (6%)
  local copies, waits for them, and re-layouts  11.6 us (5%)
  matrix products  11.1 us (5%)
  starting transfers between devices  6.9 us (3%)
    all_to_all x1, blocking collectives, sent_and_summed(): lax.all_to_all(blocks, axis, split_axis=0, concat_axis=0, tiled=True)  60.9 us
    all_gather x1, waiting for transfers between devices, body(): w_full = lax.all_gather(out_weight, 'dp', axis=0, tiled=True)  40 us
    psum x2, blocking collectives, by_axis(): array = lax.psum(array, axis)  35.1 us
    all_to_all x1, blocking collectives, body(): lax.all_to_all(hidden, 'dp', split_axis=1, concat_axis=0, tiled=True)  31.3 us
    all_to_all x1, waiting for transfers between devices, from_everyone(): lax.all_to_all(jnp.broadcast_to(array[None], (peers, *array.shape)), axis...  15.8 us
    all_gather x1, waiting for transfers between devices, body(): hidden_grad = lax.all_gather(share, VOCAB, axis=1, tiled=True)  14.7 us
    all_to_all x1, starting transfers between devices, from_everyone(): lax.all_to_all(jnp.broadcast_to(array[None], (peers, *array.shape)), axis...  6.83 us
  transfers between devices with their start and end apart: 3, of which 3 were waited for; matrix products, arithmetic and copies ran while one was open for 2% of the time, Pallas kernels for 0%

commit v1 on v0

--- a/solution.py
+++ b/solution.py
@@ -3,6 +3,7 @@
 from jax import lax
 from jax.sharding import Mesh
 from jax.sharding import PartitionSpec as P
+from jax.lax import all_to_all, axis_size
 
 VOCAB = ("vocab_0", "vocab_1")
 softcap = 30.0
@@ -70,7 +71,9 @@
         logit_grad, w_full, contract_cols, preferred_element_type=jnp.float32
     )
     share = sent_and_summed(partial_grad.astype(jnp.bfloat16), VOCAB, 1).astype(jnp.bfloat16)
-    hidden_grad = lax.all_gather(share, VOCAB, axis=1, tiled=True)
+    y2 = jnp.stack(tuple((share for _ in range(axis_size(VOCAB)))), axis=0)
+    current_block = all_to_all(y2, VOCAB, 0, 0)
+    hidden_grad = jnp.concatenate(current_block, axis=1)
     owned_cols = lax.all_to_all(hidden, "dp", split_axis=1, concat_axis=0, tiled=True)
     every_grad = gather_directly(logit_grad, "dp", 0)
     block_count = owned_cols.shape[0] // tok_rows

time: 244 us -> 271 us (1.11)
  the two profiles are of different devices: /device:TPU:4 before, /device:TPU:8 now
where the time goes in v1:
time: 271 us
  waiting for transfers between devices  120 us (44%)
  blocking collectives  95.4 us (35%)
  starting transfers between devices  16.1 us (6%)
  between operations  14.1 us (5%)
  local copies, waits for them, and re-layouts  12.8 us (5%)
  matrix products  11.2 us (4%)
    all_to_all x1, blocking collectives, sent_and_summed(): lax.all_to_all(blocks, axis, split_axis=0, concat_axis=0, tiled=True)  60.6 us
    all_to_all x1, waiting for transfers between devices, body(): current_block = all_to_all(y2, VOCAB, 0, 0)  55.6 us
    all_gather x1, waiting for transfers between devices, body(): w_full = lax.all_gather(out_weight, 'dp', axis=0, tiled=True)  44.7 us
    psum x2, blocking collectives, by_axis(): array = lax.psum(array, axis)  34.8 us
    all_to_all x1, waiting for transfers between devices, from_everyone(): lax.all_to_all(jnp.broadcast_to(array[None], (peers, *array.shape)), axis...  19 us
    all_to_all x1, starting transfers between devices, body(): current_block = all_to_all(y2, VOCAB, 0, 0)  7.29 us
  transfers between devices with their start and end apart: 4, of which 3 were waited for; matrix products, arithmetic and copies ran while one was open for 6% of the time, Pallas kernels for 0%

profile of v1, /device:TPU:8, one launch (start us, length us, event | category | flops | bytes accessed | tf_op | source)
XLA Modules:
  0.0 270.7 jit_solution(12100633851488717122)
XLA Ops:
  7.2 0.0 all-gather.2.cloned.1.call-start
  7.2 0.7 all-gather.2.cloned.1.call-update
  7.9 3.6 %all_to_all.24 = bf16[224,8,576]{2,1,0:T(8,128)(2,1)S(1)} reshape(bf16[224,4608]{1,0:T(8,128)(2,1)} %param.4) | data formatting | bytes 4128768 | tf_op jit(solution)/shard_map/all_to_all | solution.py:77
  11.5 1.7 copy.8
  13.1 4.5 %all-to-all-start.3 = ((bf16[224,8,576]{2,0,1:T(8,128)(2,1)}), bf16[224,8,576]{2,0,1:T(8,128)(2,1)}, u32[]{:S(2)}, u32[]{:S(2)}) async-start(bf16[224,8,576]{2,0,1:T(8,128)(2,1)} %copy.8), calls=%async_computation.3 | async-start | bytes 4587520 | tf_op jit(solution)/shard_map/all_to_all | solution.py:77
  17.6 0.0 copy-start.2
  17.7 44.7 %all-gather.2.cloned.1.call-done = bf16[4608,384]{1,0:T(8,128)(2,1)} async-done(((bf16[576,384]{1,0:T(8,128)(2,1)}), bf16[4608,384]{1,0:T(8,128)(2,1)}) %all-gather.2.cloned.1.call-update) | async-done | bytes 3538960 | tf_op jit(solution)/shard_map/all_gather | solution.py:55
  62.4 3.4 %fusion.7 = (f32[224]{0:T(256)S(1)}, f32[224]{0:T(256)S(1)}, f32[224,384]{1,0:T(8,128)S(1)}) fusion(pred[384]{0:T(512)(128)(4,1)S(1)} %broadcast_compare_fusion, s32[224]{0:T(256)S(1)} %copy-done.1, s32[384]{0:T(512)S(1)} %iota_add_fusion, bf16[224,4608]{1,0:T(8,128)(2,1)S(1)} %copy-done, bf16[4608,384]{1,0:T(8,128)(2,1)} %all-gather.2.cloned.1.call-done), kind=kOutput, calls=%fused_computation.13 | convolution fusion | flops 793325056 | bytes 5952000 | tf_op jit(solution)/shard_map/dot_general | solution.py:56
  65.8 16.1 %all-reduce.1 = (f32[224]{0:T(256)S(1)}, f32[224]{0:T(256)S(1)}) all-reduce(f32[224]{0:T(256)S(1)} %get-tuple-element.7, f32[224]{0:T(256)S(1)} %get-tuple-element.6), channel_id=1, replica_groups=mesh['dp'=8,'vocab_0'=8,'vocab_1'=8] {'vocab_0'}, use_global_device_ids=true, to_apply=%region_4.5 | all-reduce | flops 448 | bytes 3584 | tf_op jit(solution)/shard_map/psum | solution.py:14
  81.9 18.6 %all-reduce = (f32[224]{0:T(256)S(1)}, f32[224]{0:T(256)S(1)}) all-reduce(f32[224]{0:T(256)S(1)} %get-tuple-element.10, f32[224]{0:T(256)S(1)} %get-tuple-element.11), channel_id=1, replica_groups=mesh['dp'=8,'vocab_0'=8,'vocab_1'=8] {'vocab_1'}, use_global_device_ids=true, to_apply=%region_5.6 | all-reduce | flops 448 | bytes 3584 | tf_op jit(solution)/shard_map/psum | solution.py:14
  100.5 0.2 fusion.6
  100.7 3.4 %convolution_convert_fusion = bf16[224,4608]{1,0:T(8,128)(2,1)S(1)} fusion(bf16[224,384]{1,0:T(8,128)(2,1)S(1)} %fusion.6, bf16[4608,384]{1,0:T(8,128)(2,1)} %all-gather.2.cloned.1.call-done), kind=kOutput, calls=%fused_computation | convolution fusion | flops 793755648 | bytes 5775360 | tf_op jit(solution)/shard_map/dot_general | solution.py:70
  104.1 2.4 copy.7
  106.6 60.6 %all_to_all.31 = bf16[64,224,72]{1,2,0:T(8,128)(2,1)S(1)} all-to-all(bf16[64,224,72]{1,2,0:T(8,128)(2,1)} %bitcast.16), channel_id=1, replica_groups=mesh['dp'=8,'vocab_0'=8,'vocab_1'=8] {'vocab_0','vocab_1'}, dimensions={0} | all-to-all | bytes 4128768 | tf_op jit(solution)/shard_map/all_to_all | solution.py:25
  167.2 1.2 broadcast_in_dim.34
  168.4 4.3 %all-to-all-start.2 = ((bf16[8,224,384]{2,1,0:T(8,128)(2,1)}), bf16[8,224,384]{2,1,0:T(8,128)(2,1)}, u32[]{:S(2)}, u32[]{:S(2)}) async-start(bf16[8,224,384]{2,1,0:T(8,128)(2,1)} %broadcast_in_dim.34), calls=%async_computation.2 | async-start | bytes 2752512 | tf_op jit(solution)/shard_map/all_to_all | solution.py:31
  172.7 0.4 reduce_sum.46
  173.1 19.0 %all-to-all-done.2 = bf16[8,224,384]{2,1,0:T(8,128)(2,1)} async-done(((bf16[8,224,384]{2,1,0:T(8,128)(2,1)}), bf16[8,224,384]{2,1,0:T(8,128)(2,1)}, u32[]{:S(2)}, u32[]{:S(2)}) %all-to-all-start.2) | async-done | bytes 1376288 | tf_op jit(solution)/shard_map/all_to_all | solution.py:31
  192.2 1.6 stack.2
  193.7 7.3 %all-to-all-start.1 = ((bf16[64,224,72]{1,2,0:T(8,128)(2,1)}), bf16[64,224,72]{1,2,0:T(8,128)(2,1)S(1)}, u32[]{:S(2)}, u32[]{:S(2)}) async-start(bf16[64,224,72]{1,2,0:T(8,128)(2,1)} %stack.2), calls=%async_computation.1 | async-start | bytes 4718592 | tf_op jit(solution)/shard_map/all_to_all | solution.py:75
  201.0 0.6 log_subtract_fusion
  201.6 4.4 %convert_reduce_fusion = bf16[384,576]{0,1:T(8,128)(2,1)} fusion(bf16[8,224,384]{2,1,0:T(8,128)(2,1)} %all-to-all-done.2, bf16[224,8,576]{2,0,1:T(8,128)(2,1)} %all-to-all-done.3), kind=kOutput, calls=%fused_computation.1 | convolution fusion | flops 796041216 | bytes 3883008 | tf_op jit(solution)/shard_map/ntr,ntv->nrv/dot_general | solution.py:82
  206.0 55.6 %all-to-all-done.1 = bf16[64,224,72]{1,2,0:T(8,128)(2,1)S(1)} async-done(((bf16[64,224,72]{1,2,0:T(8,128)(2,1)}), bf16[64,224,72]{1,2,0:T(8,128)(2,1)S(1)}, u32[]{:S(2)}, u32[]{:S(2)}) %all-to-all-start.1) | async-done | bytes 2064416 | tf_op jit(solution)/shard_map/all_to_all | solution.py:75
  261.5 2.3 copy.9
  (8 shorter events, 0.0 us)
Async XLA Ops:
  7.2 55.2 %all-gather.2.cloned.1.call-start = ((), (), s32[]{:S(2)}) async-start(), calls=%async_computation.4 | async-start | bytes 3981312 | tf_op jit(solution)/shard_map/all_gather | solution.py:55
  13.1 49.2 %copy-start = (bf16[224,4608]{1,0:T(8,128)(2,1)S(1)}, bf16[224,4608]{1,0:T(8,128)(2,1)}, u32[]{:S(2)}) copy-start(bf16[224,4608]{1,0:T(8,128)(2,1)} %param.4) | copy-start | bytes 6193156
  13.1 49.2 %copy-start.1 = (s32[224]{0:T(256)S(1)}, s32[224]{0:T(256)}, u32[]{:S(2)}) copy-start(s32[224]{0:T(256)} %param.6) | copy-start | bytes 2692
  13.1 93.5 %all-to-all-start.3 = ((bf16[224,8,576]{2,0,1:T(8,128)(2,1)}), bf16[224,8,576]{2,0,1:T(8,128)(2,1)}, u32[]{:S(2)}, u32[]{:S(2)}) async-start(bf16[224,8,576]{2,0,1:T(8,128)(2,1)} %copy.8), calls=%async_computation.3 | async-start | bytes 4587520 | tf_op jit(solution)/shard_map/all_to_all | solution.py:77
  17.6 82.9 %copy-start.2 = (f32[224]{0:T(256)S(1)}, f32[224]{0:T(256)}, u32[]{:S(2)}) copy-start(f32[224]{0:T(256)} %param.7) | copy-start | bytes 2692
  168.4 23.7 %all-to-all-start.2 = ((bf16[8,224,384]{2,1,0:T(8,128)(2,1)}), bf16[8,224,384]{2,1,0:T(8,128)(2,1)}, u32[]{:S(2)}, u32[]{:S(2)}) async-start(bf16[8,224,384]{2,1,0:T(8,128)(2,1)} %broadcast_in_dim.34), calls=%async_computation.2 | async-start | bytes 2752512 | tf_op jit(solution)/shard_map/all_to_all | solution.py:31
  193.7 67.8 %all-to-all-start.1 = ((bf16[64,224,72]{1,2,0:T(8,128)(2,1)}), bf16[64,224,72]{1,2,0:T(8,128)(2,1)S(1)}, u32[]{:S(2)}, u32[]{:S(2)}) async-start(bf16[64,224,72]{1,2,0:T(8,128)(2,1)} %stack.2), calls=%async_computation.1 | async-start | bytes 4718592 | tf_op jit(solution)/shard_map/all_to_all | solution.py:75
Sparse Core Ops, SparseCore 0:
  10.1 52.2 all-gather.1
